TPU v7x, 32 devices: a whole 2x2x4 slice. The times are simulated.
32 devices in a mesh: grp: 8 (over z, y), mem: 4 (over x, core).
Axes of the slice: x: 2, y: 2, z: 4, core: 2. Of those that a mesh axis runs over, the one named last changes fastest.
Arguments:
- queries: bfloat16 [8192, 2048], P(('grp', 'mem')), may hold values from -6 to 6
- keys: bfloat16 [8192, 2048], P(('grp', 'mem')), may hold values from -6 to 6
- values: bfloat16 [8192, 2048], P(('grp', 'mem')), may hold values from -6 to 6
- grad_out: bfloat16 [8192, 2048], P(('grp', 'mem')), may hold values from -0.125 to 0.125
- log_decay: float32 [8, 8192], P(None, ('grp', 'mem')), may hold values from -1.6 to 0
Outputs:
- grad_queries: bfloat16 [8192, 2048], P(('grp', 'mem'))
- grad_keys: bfloat16 [8192, 2048], P(('grp', 'mem'))
- grad_values: bfloat16 [8192, 2048], P(('grp', 'mem'))
All inputs are finite; a program needn't handle non-finite values.
Results may differ from a plain program's by a relative error of at most 0.0052.
Values sent between devices are 32-bit elements; how exact they have to be, the bound alone decides.
A program may use at most 128 MiB of HBM per device.

v0:
```python
import jax
import jax.numpy as jnp
from jax import lax
from jax.sharding import PartitionSpec as P

HEAD_COUNT = 8
DK = 256
DV = 256
BLOCK = 128


def prefix(value, axis, join, neutral, backward):
    count, mine = (lax.axis_size(axis), lax.axis_index(axis))
    pieces = jax.tree.map(lambda part: lax.all_gather(part, axis), value)
    if backward:
        pieces = jax.tree.map(lambda part: part[::-1], pieces)
        mine = count - 1 - mine
    total = jax.tree.map(
        lambda part, zero: jnp.full_like(part, 0) + jnp.asarray(zero, part.dtype), value, neutral
    )

    def turn(position, total):
        longer = join(total, jax.tree.map(lambda part: part[position], pieces))
        return jax.tree.map(lambda new, old: jnp.where(position < mine, new, old), longer, total)

    return lax.fori_loop(0, count - 1, turn, total)


def chain(earlier, later):
    early_decay, early_state = earlier
    late_decay, late_state = later
    return (early_decay * late_decay, late_state + late_decay[:, None, None] * early_state)


def body(queries, keys, values, grad_out, log_decay):
    tokens = queries.shape[0]
    count = tokens // BLOCK
    scale = DK ** (-0.5)
    query_blocks = queries.reshape(count, BLOCK, HEAD_COUNT, DK)
    key_blocks = keys.reshape(count, BLOCK, HEAD_COUNT, DK)
    value_blocks = values.reshape(count, BLOCK, HEAD_COUNT, DV)
    grad_blocks = grad_out.reshape(count, BLOCK, HEAD_COUNT, DV)
    logs = jnp.transpose(log_decay.reshape(HEAD_COUNT, count, BLOCK), (1, 0, 2))
    cumul = jnp.cumsum(logs, axis=2)
    ends = cumul[:, :, -1]
    lower = jnp.tril(jnp.ones((BLOCK, BLOCK), dtype=bool))
    spread = cumul[:, :, :, None] - cumul[:, :, None, :]
    decay = jnp.where(lower, jnp.exp(jnp.where(lower, spread, 0.0)), 0.0)
    scores = jnp.einsum(
        "bthe,bshe->bhts", grad_blocks, value_blocks, preferred_element_type=jnp.float32
    )
    weight_grad = (scores * decay).astype(jnp.bfloat16)
    attend = jnp.einsum(
        "bthd,bshd->bhts", query_blocks, key_blocks, preferred_element_type=jnp.float32
    )
    weight_value = (attend * decay).astype(jnp.bfloat16)
    inner_query = jnp.einsum(
        "bhts,bshd->bthd", weight_grad, key_blocks, preferred_element_type=jnp.float32
    )
    inner_key = jnp.einsum(
        "bhts,bthd->bshd", weight_grad, query_blocks, preferred_element_type=jnp.float32
    )
    inner_value = jnp.einsum(
        "bhts,bthe->bshe", weight_value, grad_blocks, preferred_element_type=jnp.float32
    )
    head_factor = jnp.exp(jnp.transpose(cumul, (0, 2, 1)))[..., None]
    tail_factor = jnp.exp(jnp.transpose(ends[:, :, None] - cumul, (0, 2, 1)))[..., None]
    keys_decayed = (key_blocks * tail_factor).astype(jnp.bfloat16)
    queries_decayed = (query_blocks * head_factor).astype(jnp.bfloat16)
    forward_parts = jnp.einsum(
        "bshd,bshe->bhde", keys_decayed, value_blocks, preferred_element_type=jnp.float32
    )
    reverse_parts = jnp.einsum(
        "bthd,bthe->bhde", queries_decayed, grad_blocks, preferred_element_type=jnp.float32
    )
    block_decay = jnp.exp(ends)
    running = jnp.zeros((HEAD_COUNT, DK, DV), jnp.float32)
    carried = jnp.ones((HEAD_COUNT,), jnp.float32)
    prefix_list = []
    carried_list = []
    for position in range(count):
        prefix_list.append(running)
        carried_list.append(carried)
        running = block_decay[position][:, None, None] * running + forward_parts[position]
        carried = carried * block_decay[position]
    forward_total = running
    running = jnp.zeros((HEAD_COUNT, DK, DV), jnp.float32)
    after = jnp.ones((HEAD_COUNT,), jnp.float32)
    suffix_list = [None] * count
    after_list = [None] * count
    for position in reversed(range(count)):
        suffix_list[position] = running
        after_list[position] = after
        running = block_decay[position][:, None, None] * running + reverse_parts[position]
        after = after * block_decay[position]
    members = lax.axis_size("mem")
    decay_cols = jnp.broadcast_to(carried[None, :, None, None], (1, HEAD_COUNT, members, 1))
    pieces = (
        lax.all_to_all(decay_cols, "mem", split_axis=2, concat_axis=0, tiled=True),
        lax.all_to_all(forward_total[None], "mem", split_axis=2, concat_axis=0, tiled=True),
        lax.all_to_all(running[None], "mem", split_axis=2, concat_axis=0, tiled=True),
    )
    member_decays = pieces[0][:, :, 0, 0]
    width = DK // members
    share_identity = (
        jnp.ones((HEAD_COUNT,), jnp.float32),
        jnp.zeros((HEAD_COUNT, width, DV), jnp.float32),
    )
    forward_prefix = []
    accum = share_identity
    for index in range(members):
        forward_prefix.append(accum)
        accum = chain(accum, (member_decays[index], pieces[1][index]))
    forward_whole = accum
    reverse_prefix = [None] * members
    accum = share_identity
    for index in reversed(range(members)):
        reverse_prefix[index] = accum
        accum = chain(accum, (member_decays[index], pieces[2][index]))
    group_first = prefix(forward_whole, "grp", chain, share_identity, False)
    group_second = prefix(accum, "grp", chain, share_identity, True)
    first_stack = jnp.stack(
        [chain(group_first, forward_prefix[index])[1] for index in range(members)]
    )
    second_stack = jnp.stack(
        [chain(group_second, reverse_prefix[index])[1] for index in range(members)]
    )
    returned = (
        lax.all_to_all(first_stack, "mem", split_axis=0, concat_axis=2, tiled=True),
        lax.all_to_all(second_stack, "mem", split_axis=0, concat_axis=2, tiled=True),
    )
    state_from = returned[0][0]
    grads_from = returned[1][0]
    states_low = (
        jnp.stack(prefix_list) + jnp.stack(carried_list)[:, :, None, None] * state_from[None]
    ).astype(jnp.bfloat16)
    grads_low = (
        jnp.stack(suffix_list) + jnp.stack(after_list)[:, :, None, None] * grads_from[None]
    ).astype(jnp.bfloat16)
    outer_query = jnp.einsum(
        "bthe,bhde->bthd", grad_blocks, states_low, preferred_element_type=jnp.float32
    )
    outer_key = jnp.einsum(
        "bshe,bhde->bshd", value_blocks, grads_low, preferred_element_type=jnp.float32
    )
    outer_value = jnp.einsum(
        "bshd,bhde->bshe", key_blocks, grads_low, preferred_element_type=jnp.float32
    )
    grad_queries = (scale * (inner_query + head_factor * outer_query)).astype(jnp.bfloat16)
    grad_keys = (scale * (inner_key + tail_factor * outer_key)).astype(jnp.bfloat16)
    grad_values = (scale * (inner_value + tail_factor * outer_value)).astype(jnp.bfloat16)
    return (
        grad_queries.reshape(tokens, HEAD_COUNT * DK),
        grad_keys.reshape(tokens, HEAD_COUNT * DK),
        grad_values.reshape(tokens, HEAD_COUNT * DV),
    )


def solution(mesh):
    placed = (
        P(("grp", "mem"), None),
        P(("grp", "mem"), None),
        P(("grp", "mem"), None),
        P(("grp", "mem"), None),
        P(None, ("grp", "mem")),
    )
    return jax.shard_map(
        body,
        mesh=mesh,
        in_specs=placed,
        out_specs=(P(("grp", "mem"), None), P(("grp", "mem"), None), P(("grp", "mem"), None)),
        check_vma=False,
    )
```

profile of v0, /device:TPU:0, one launch (start us, length us, event | category | flops | bytes accessed | tf_op | source)
XLA Modules:
  0.0 301.0 jit_solution(9682326019785282810)
XLA Ops:
  9.3 4.2 %all-to-all-start.1 = ((f32[1,8,4,1]{1,3,0,2:T(1,128)}), f32[1,8,4,1]{1,3,0,2:T(1,128)S(1)}, u32[]{:S(2)}, u32[]{:S(2)}) async-start(f32[1,8,4,1]{1,3,0,2:T(1,128)} %broadcast_in_dim.21), calls=%async_computation.1 | async-start | bytes 4096 | tf_op jit(solution)/shard_map/all_to_all | solution.py:99
  13.6 1.6 copy.135
  20.3 2.9 slice_add_fusion
  23.2 2.6 copy.103
  25.8 4.5 %all-to-all-start.3 = ((f32[1,8,256,256]{3,1,0,2:T(8,128)}), f32[1,8,256,256]{3,1,0,2:T(8,128)}, u32[]{:S(2)}, u32[]{:S(2)}) async-start(f32[1,8,256,256]{3,1,0,2:T(8,128)} %copy.103), calls=%async_computation.3 | async-start | bytes 4194304 | tf_op jit(solution)/shard_map/all_to_all | solution.py:101
  30.3 4.1 %copy.89 = f32[1,8,256,256]{3,1,0,2:T(8,128)} copy(f32[1,8,256,256]{3,2,1,0:T(8,128)} %get-tuple-element.284) | data formatting | bytes 4194304 | tf_op jit(solution)/shard_map/add | solution.py:84
  34.4 21.6 %all-to-all-done.3 = f32[1,8,256,256]{3,1,0,2:T(8,128)} async-done(((f32[1,8,256,256]{3,1,0,2:T(8,128)}), f32[1,8,256,256]{3,1,0,2:T(8,128)}, u32[]{:S(2)}, u32[]{:S(2)}) %all-to-all-start.3) | async-done | bytes 2097184 | tf_op jit(solution)/shard_map/all_to_all | solution.py:101
  56.0 4.4 %all-to-all-start = ((f32[1,8,256,256]{3,1,0,2:T(8,128)}), f32[1,8,256,256]{3,1,0,2:T(8,128)}, u32[]{:S(2)}, u32[]{:S(2)}) async-start(f32[1,8,256,256]{3,1,0,2:T(8,128)} %copy.89), calls=%async_computation | async-start | bytes 4194304 | tf_op jit(solution)/shard_map/all_to_all | solution.py:100
  60.5 3.6 %copy.173 = f32[1,8,4,64,256]{4,3,1,0,2:T(8,128)} copy(f32[1,8,4,64,256]{4,1,3,2,0:T(8,128)} %bitcast.39) | data formatting | bytes 4194304 | tf_op jit(solution)/shard_map/all_to_all | solution.py:101
  64.1 22.1 %all-to-all-done = f32[1,8,256,256]{3,1,0,2:T(8,128)} async-done(((f32[1,8,256,256]{3,1,0,2:T(8,128)}), f32[1,8,256,256]{3,1,0,2:T(8,128)}, u32[]{:S(2)}, u32[]{:S(2)}) %all-to-all-start) | async-done | bytes 2097184 | tf_op jit(solution)/shard_map/all_to_all | solution.py:100
  86.2 2.4 copy.90
  88.6 1.7 fusion.38
  91.1 21.7 %all-gather.1 = f32[8,1,8]{2,1,0:T(1,128)S(1)} all-gather(f32[1,1,8]{2,1,0:T(1,128)S(1)} %get-tuple-element.269), channel_id=1, replica_groups=mesh['grp'=8,'mem'=4] {'grp'}, dimensions={0}, use_global_device_ids=true | all-gather | bytes 288 | tf_op jit(solution)/shard_map/all_gather | solution.py:14
  112.8 16.6 %all-gather = f32[8,1,8]{2,1,0:T(1,128)S(1)} all-gather(f32[1,1,8]{2,1,0:T(1,128)S(1)} %get-tuple-element.270), channel_id=1, replica_groups=mesh['grp'=8,'mem'=4] {'grp'}, dimensions={0}, use_global_device_ids=true | all-gather | bytes 288 | tf_op jit(solution)/shard_map/all_gather | solution.py:14
  129.4 34.7 %all-gather.7.cloned.1.call-done = f32[8,8,64,256]{3,2,1,0:T(8,128)} async-done(((f32[1,8,64,256]{3,2,1,0:T(8,128)}), f32[8,8,64,256]{3,2,1,0:T(8,128)}) %all-gather.7.cloned.1.call-update) | async-done | bytes 4194320 | tf_op jit(solution)/shard_map/all_gather | solution.py:14
  164.1 4.7 %rev.6 = f32[8,8,64,256]{3,2,1,0:T(8,128)} reverse(f32[8,8,64,256]{3,2,1,0:T(8,128)} %all-gather.7.cloned.1.call-done), dimensions={0} | reverse | bytes 8388608 | tf_op jit(solution)/shard_map/rev | solution.py:16
  168.8 8.5 %while.29 = (s32[]{:T(128)}, f32[8,64,256]{2,1,0:T(8,128)S(1)}, s32[]{:T(128)}, f32[8,8,64,256]{3,2,1,0:T(8,128)}, f32[8,8]{1,0:T(8,128)S(1)}, /*index=5*/s32[]{:T(128)}, s32[]{:T(128)}) while((s32[]{:T(128)}, f32[8,64,256]{2,1,0:T(8,128)S(1)}, s32[]{:T(128)}, f32[8,8,64,256]{3,2,1,0:T(8,128)}, f32[8,8]{1,0:T(8,128)S(1)}, ...), condition=%wide.region_4.5_spmd.clone, body=%wide.region_3.4_spmd.clone.sunk | while | flops 524292 | bytes 1573073 | solution.py:26
  177.4 1.7 fusion.51
  179.1 1.6 pad_maximum_fusion.1
  180.6 4.4 %all-to-all-start.4 = ((f32[4,8,64,256]{3,2,1,0:T(8,128)}), f32[4,8,64,256]{3,2,1,0:T(8,128)}, u32[]{:S(2)}, u32[]{:S(2)}) async-start(f32[4,8,64,256]{3,2,1,0:T(8,128)} %pad_maximum_fusion.1), calls=%async_computation.4 | async-start | bytes 4194304 | tf_op jit(solution)/shard_map/all_to_all | solution.py:130
  185.1 52.5 %all-gather.5.cloned.1.call-done = f32[8,8,64,256]{3,2,1,0:T(8,128)} async-done(((f32[1,8,64,256]{3,2,1,0:T(8,128)}), f32[8,8,64,256]{3,2,1,0:T(8,128)}) %all-gather.5.cloned.1.call-update) | async-done | bytes 4194320 | tf_op jit(solution)/shard_map/all_gather | solution.py:14
  237.6 8.5 %while.28 = (s32[]{:T(128)}, f32[8,64,256]{2,1,0:T(8,128)S(1)}, s32[]{:T(128)}, f32[8,8,64,256]{3,2,1,0:T(8,128)}, f32[8,8]{1,0:T(8,128)S(1)}, /*index=5*/s32[]{:T(128)}, s32[]{:T(128)}) while((s32[]{:T(128)}, f32[8,64,256]{2,1,0:T(8,128)S(1)}, s32[]{:T(128)}, f32[8,8,64,256]{3,2,1,0:T(8,128)}, f32[8,8]{1,0:T(8,128)S(1)}, ...), condition=%wide.region_2.3_spmd.clone, body=%wide.region_1.2_spmd.clone.sunk | while | flops 524292 | bytes 1573073 | solution.py:26
  246.1 1.7 add_bitcast_fusion.2
  249.3 4.8 %all-to-all-start.2 = ((f32[4,8,64,256]{3,2,1,0:T(8,128)}), f32[4,8,64,256]{3,2,1,0:T(8,128)}, u32[]{:S(2)}, u32[]{:S(2)}) async-start(f32[4,8,64,256]{3,2,1,0:T(8,128)} %pad_maximum_fusion), calls=%async_computation.2 | async-start | bytes 4194304 | tf_op jit(solution)/shard_map/all_to_all | solution.py:129
  254.1 2.7 fusion.14
  256.8 1.8 copy.106
  258.7 2.3 fusion.24
  261.0 2.1 fusion.28
  263.1 16.5 %all-to-all-done.2 = f32[4,8,64,256]{3,2,1,0:T(8,128)} async-done(((f32[4,8,64,256]{3,2,1,0:T(8,128)}), f32[4,8,64,256]{3,2,1,0:T(8,128)}, u32[]{:S(2)}, u32[]{:S(2)}) %all-to-all-start.2) | async-done | bytes 2097184 | tf_op jit(solution)/shard_map/all_to_all | solution.py:129
  279.6 1.9 copy.94
  287.9 3.2 %fusion.5 = bf16[2,128,8,256]{3,1,2,0:T(8,128)(2,1)} fusion(f32[2,8,256,128]{2,3,1,0:T(8,128)} %fusion.28, f32[2,128,8]{1,2,0:T(8,128)S(1)} %get-tuple-element.264, bf16[2,128,8,256]{3,2,1,0:T(8,128)(2,1)S(1)} %bitcast.295, bf16[2,128,8,256]{3,2,1,0:T(8,128)(2,1)S(1)} %bitcast.288, bf16[2,128,8,256]{3,2,1,0:T(8,128)(2,1)S(1)} %bitcast.299, ...), kind=kOutput, calls=%fused_computation.18 | convolution fusion | flops 271843328 | bytes 6324224 | tf_op jit(solution)/shard_map/bhts,bthe->bshe/dot_general | solution.py:63
  291.1 1.8 copy.117
  (98 shorter events, 33.8 us)
Async XLA Ops:
  7.2 8.1 %copy-start.14 = (bf16[256,2048]{1,0:T(8,128)(2,1)S(1)}, bf16[256,2048]{1,0:T(8,128)(2,1)}, u32[]{:S(2)}) copy-start(bf16[256,2048]{1,0:T(8,128)(2,1)} %param.12) | copy-start | bytes 3145732
  9.3 16.5 %all-to-all-start.1 = ((f32[1,8,4,1]{1,3,0,2:T(1,128)}), f32[1,8,4,1]{1,3,0,2:T(1,128)S(1)}, u32[]{:S(2)}, u32[]{:S(2)}) async-start(f32[1,8,4,1]{1,3,0,2:T(1,128)} %broadcast_in_dim.21), calls=%async_computation.1 | async-start | bytes 4096 | tf_op jit(solution)/shard_map/all_to_all | solution.py:99
  13.6 2.0 copy-start.15
  15.2 2.4 copy-start.4
  15.2 2.0 copy-start.16
  15.6 2.0 copy-start.6
  15.9 3.1 %copy-start.9 = (bf16[32,8,8,256]{3,2,1,0:T(8,128)(2,1)}, bf16[32,8,8,256]{3,2,1,0:T(8,128)(2,1)S(1)}, u32[]{:S(2)}) copy-start(bf16[32,8,8,256]{3,2,1,0:T(8,128)(2,1)S(1)} %copy.132) | copy-start | bytes 3145732
  17.6 1.4 copy-start
  25.8 30.2 %all-to-all-start.3 = ((f32[1,8,256,256]{3,1,0,2:T(8,128)}), f32[1,8,256,256]{3,1,0,2:T(8,128)}, u32[]{:S(2)}, u32[]{:S(2)}) async-start(f32[1,8,256,256]{3,1,0,2:T(8,128)} %copy.103), calls=%async_computation.3 | async-start | bytes 4194304 | tf_op jit(solution)/shard_map/all_to_all | solution.py:101
  56.0 30.2 %all-to-all-start = ((f32[1,8,256,256]{3,1,0,2:T(8,128)}), f32[1,8,256,256]{3,1,0,2:T(8,128)}, u32[]{:S(2)}, u32[]{:S(2)}) async-start(f32[1,8,256,256]{3,1,0,2:T(8,128)} %copy.89), calls=%async_computation | async-start | bytes 4194304 | tf_op jit(solution)/shard_map/all_to_all | solution.py:100
  60.4 103.7 %all-gather.7.cloned.1.call-start = ((), (), s32[]{:S(2)}) async-start(), calls=%async_computation.6 | async-start | bytes 4718592 | tf_op jit(solution)/shard_map/all_gather | solution.py:14
  86.2 2.4 copy-start.3
  88.6 1.7 copy-start.2
  90.3 147.3 %all-gather.5.cloned.1.call-start = ((), (), s32[]{:S(2)}) async-start(), calls=%async_computation.5 | async-start | bytes 4718592 | tf_op jit(solution)/shard_map/all_gather | solution.py:14
  180.6 68.7 %all-to-all-start.4 = ((f32[4,8,64,256]{3,2,1,0:T(8,128)}), f32[4,8,64,256]{3,2,1,0:T(8,128)}, u32[]{:S(2)}, u32[]{:S(2)}) async-start(f32[4,8,64,256]{3,2,1,0:T(8,128)} %pad_maximum_fusion.1), calls=%async_computation.4 | async-start | bytes 4194304 | tf_op jit(solution)/shard_map/all_to_all | solution.py:130
  249.3 4.8 %copy-start.7 = (bf16[32,8,8,256]{3,2,1,0:T(8,128)(2,1)S(1)}, bf16[32,8,8,256]{3,2,1,0:T(8,128)(2,1)}, u32[]{:S(2)}) copy-start(bf16[32,8,8,256]{3,2,1,0:T(8,128)(2,1)} %copy-done.6) | copy-start | bytes 3145732
  249.3 30.3 %all-to-all-start.2 = ((f32[4,8,64,256]{3,2,1,0:T(8,128)}), f32[4,8,64,256]{3,2,1,0:T(8,128)}, u32[]{:S(2)}, u32[]{:S(2)}) async-start(f32[4,8,64,256]{3,2,1,0:T(8,128)} %pad_maximum_fusion), calls=%async_computation.2 | async-start | bytes 4194304 | tf_op jit(solution)/shard_map/all_to_all | solution.py:129
  256.8 1.9 copy-start.10
  258.7 2.3 copy-start.1
  263.1 18.4 %copy-start.8 = (bf16[32,8,8,256]{3,2,1,0:T(8,128)(2,1)S(1)}, bf16[32,8,8,256]{3,2,1,0:T(8,128)(2,1)}, u32[]{:S(2)}) copy-start(bf16[32,8,8,256]{3,2,1,0:T(8,128)(2,1)} %copy-done.6) | copy-start | bytes 3145732
  279.6 2.2 copy-start.11
  281.8 1.0 copy-start.13
  283.4 1.9 copy-start.5
  283.4 1.9 copy-start.12
Sparse Core Ops, SparseCore 0:
  90.4 73.6 all-gather.6
  166.2 71.3 all-gather.4
where the time goes:
time: 303 us; the launch traced here: 301 us
  waiting for transfers between devices  148 us (49%)
  blocking collectives  38.3 us (13%)
  local copies, waits for them, and re-layouts  33.3 us (11%)
  other arithmetic  28.9 us (10%)
  starting transfers between devices  22.4 us (7%)
  matrix products  15 us (5%)
  between operations  14.4 us (5%)
    all_gather x2, waiting for transfers between devices, prefix(): pieces = jax.tree.map(lambda part: lax.all_gather(part, axis), value)  87.2 us
    all_gather x2, blocking collectives, prefix(): pieces = jax.tree.map(lambda part: lax.all_gather(part, axis), value)  38.3 us
    all_to_all x1, waiting for transfers between devices, body(): lax.all_to_all(forward_total[None], 'mem', split_axis=2, concat_axis=0, t...  22.1 us
    all_to_all x1, waiting for transfers between devices, body(): lax.all_to_all(running[None], 'mem', split_axis=2, concat_axis=0, tiled=T...  21.6 us
    all_to_all x1, waiting for transfers between devices, body(): lax.all_to_all(first_stack, 'mem', split_axis=0, concat_axis=2, tiled=True)  16.5 us
    select_n x14, other arithmetic, turn(): jnp.where(position < mine, new, old)  16.5 us
    unnamed x41, local copies, waits for them, and re-layouts  8.32 us
  transfers between devices with their start and end apart: 7, of which 5 were waited for; matrix products, arithmetic and copies ran while one was open for 18% of the time, Pallas kernels for 0%

commit v1 on v0

--- a/solution.py
+++ b/solution.py
@@ -126,7 +126,12 @@
         [chain(group_second, reverse_prefix[index])[1] for index in range(members)]
     )
     returned = (
-        lax.all_to_all(first_stack, "mem", split_axis=0, concat_axis=2, tiled=True),
+        jnp.concatenate(
+            lax.all_to_all(
+                jnp.stack(jnp.split(first_stack, lax.axis_size("mem"), axis=0)), "mem", 0, 0
+            ),
+            axis=2,
+        ),
         lax.all_to_all(second_stack, "mem", split_axis=0, concat_axis=2, tiled=True),
     )
     state_from = returned[0][0]

time: 303 us -> 303 us (level)
  no operation moved by 1% of the time
where the time goes in v1:
time: 303 us; the launch traced here: 301 us
  waiting for transfers between devices  148 us (49%)
  blocking collectives  38.3 us (13%)
  local copies, waits for them, and re-layouts  33.3 us (11%)
  other arithmetic  28.9 us (10%)
  starting transfers between devices  22.4 us (7%)
  matrix products  15 us (5%)
  between operations  14.4 us (5%)
    all_gather x2, waiting for transfers between devices, prefix(): pieces = jax.tree.map(lambda part: lax.all_gather(part, axis), value)  87.2 us
    all_gather x2, blocking collectives, prefix(): pieces = jax.tree.map(lambda part: lax.all_gather(part, axis), value)  38.3 us
    all_to_all x1, waiting for transfers between devices, body(): lax.all_to_all(forward_total[None], 'mem', split_axis=2, concat_axis=0, t...  22.1 us
    all_to_all x1, waiting for transfers between devices, body(): lax.all_to_all(running[None], 'mem', split_axis=2, concat_axis=0, tiled=T...  21.6 us
    all_to_all x1, waiting for transfers between devices, body(): lax.all_to_all(jnp.stack(jnp.split(first_stack, lax.axis_size('mem'), axi...  16.5 us
    select_n x14, other arithmetic, turn(): jnp.where(position < mine, new, old)  16.5 us
    unnamed x41, local copies, waits for them, and re-layouts  8.32 us
  transfers between devices with their start and end apart: 7, of which 5 were waited for; matrix products, arithmetic and copies ran while one was open for 18% of the time, Pallas kernels for 0%

profile of v1, /device:TPU:0, one launch (start us, length us, event | category | flops | bytes accessed | tf_op | source)
XLA Modules:
  0.0 301.0 jit_solution(9682326019785282810)
XLA Ops:
  9.3 4.2 %all-to-all-start.1 = ((f32[1,8,4,1]{1,3,0,2:T(1,128)}), f32[1,8,4,1]{1,3,0,2:T(1,128)S(1)}, u32[]{:S(2)}, u32[]{:S(2)}) async-start(f32[1,8,4,1]{1,3,0,2:T(1,128)} %broadcast_in_dim.21), calls=%async_computation.1 | async-start | bytes 4096 | tf_op jit(solution)/shard_map/all_to_all | solution.py:99
  13.6 1.6 copy.135
  20.3 2.9 slice_add_fusion
  23.2 2.6 copy.103
  25.8 4.5 %all-to-all-start.3 = ((f32[1,8,256,256]{3,1,0,2:T(8,128)}), f32[1,8,256,256]{3,1,0,2:T(8,128)}, u32[]{:S(2)}, u32[]{:S(2)}) async-start(f32[1,8,256,256]{3,1,0,2:T(8,128)} %copy.103), calls=%async_computation.3 | async-start | bytes 4194304 | tf_op jit(solution)/shard_map/all_to_all | solution.py:101
  30.3 4.1 %copy.89 = f32[1,8,256,256]{3,1,0,2:T(8,128)} copy(f32[1,8,256,256]{3,2,1,0:T(8,128)} %get-tuple-element.284) | data formatting | bytes 4194304 | tf_op jit(solution)/shard_map/add | solution.py:84
  34.4 21.6 %all-to-all-done.3 = f32[1,8,256,256]{3,1,0,2:T(8,128)} async-done(((f32[1,8,256,256]{3,1,0,2:T(8,128)}), f32[1,8,256,256]{3,1,0,2:T(8,128)}, u32[]{:S(2)}, u32[]{:S(2)}) %all-to-all-start.3) | async-done | bytes 2097184 | tf_op jit(solution)/shard_map/all_to_all | solution.py:101
  56.0 4.4 %all-to-all-start = ((f32[1,8,256,256]{3,1,0,2:T(8,128)}), f32[1,8,256,256]{3,1,0,2:T(8,128)}, u32[]{:S(2)}, u32[]{:S(2)}) async-start(f32[1,8,256,256]{3,1,0,2:T(8,128)} %copy.89), calls=%async_computation | async-start | bytes 4194304 | tf_op jit(solution)/shard_map/all_to_all | solution.py:100
  60.5 3.6 %copy.173 = f32[1,8,4,64,256]{4,3,1,0,2:T(8,128)} copy(f32[1,8,4,64,256]{4,1,3,2,0:T(8,128)} %bitcast.38) | data formatting | bytes 4194304 | tf_op jit(solution)/shard_map/all_to_all | solution.py:101
  64.1 22.1 %all-to-all-done = f32[1,8,256,256]{3,1,0,2:T(8,128)} async-done(((f32[1,8,256,256]{3,1,0,2:T(8,128)}), f32[1,8,256,256]{3,1,0,2:T(8,128)}, u32[]{:S(2)}, u32[]{:S(2)}) %all-to-all-start) | async-done | bytes 2097184 | tf_op jit(solution)/shard_map/all_to_all | solution.py:100
  86.2 2.4 copy.90
  88.6 1.7 fusion.38
  91.1 21.7 %all-gather.1 = f32[8,1,8]{2,1,0:T(1,128)S(1)} all-gather(f32[1,1,8]{2,1,0:T(1,128)S(1)} %get-tuple-element.269), channel_id=1, replica_groups=mesh['grp'=8,'mem'=4] {'grp'}, dimensions={0}, use_global_device_ids=true | all-gather | bytes 288 | tf_op jit(solution)/shard_map/all_gather | solution.py:14
  112.8 16.6 %all-gather = f32[8,1,8]{2,1,0:T(1,128)S(1)} all-gather(f32[1,1,8]{2,1,0:T(1,128)S(1)} %get-tuple-element.270), channel_id=1, replica_groups=mesh['grp'=8,'mem'=4] {'grp'}, dimensions={0}, use_global_device_ids=true | all-gather | bytes 288 | tf_op jit(solution)/shard_map/all_gather | solution.py:14
  129.4 34.7 %all-gather.7.cloned.1.call-done = f32[8,8,64,256]{3,2,1,0:T(8,128)} async-done(((f32[1,8,64,256]{3,2,1,0:T(8,128)}), f32[8,8,64,256]{3,2,1,0:T(8,128)}) %all-gather.7.cloned.1.call-update) | async-done | bytes 4194320 | tf_op jit(solution)/shard_map/all_gather | solution.py:14
  164.1 4.7 %rev.6 = f32[8,8,64,256]{3,2,1,0:T(8,128)} reverse(f32[8,8,64,256]{3,2,1,0:T(8,128)} %all-gather.7.cloned.1.call-done), dimensions={0} | reverse | bytes 8388608 | tf_op jit(solution)/shard_map/rev | solution.py:16
  168.8 8.5 %while.29 = (s32[]{:T(128)}, f32[8,64,256]{2,1,0:T(8,128)S(1)}, s32[]{:T(128)}, f32[8,8,64,256]{3,2,1,0:T(8,128)}, f32[8,8]{1,0:T(8,128)S(1)}, /*index=5*/s32[]{:T(128)}, s32[]{:T(128)}) while((s32[]{:T(128)}, f32[8,64,256]{2,1,0:T(8,128)S(1)}, s32[]{:T(128)}, f32[8,8,64,256]{3,2,1,0:T(8,128)}, f32[8,8]{1,0:T(8,128)S(1)}, ...), condition=%wide.region_4.5_spmd.clone, body=%wide.region_3.4_spmd.clone.sunk | while | flops 524292 | bytes 1573073 | solution.py:26
  177.4 1.7 fusion.51
  179.1 1.6 pad_maximum_fusion.1
  180.6 4.4 %all-to-all-start.4 = ((f32[4,8,64,256]{3,2,1,0:T(8,128)}), f32[4,8,64,256]{3,2,1,0:T(8,128)}, u32[]{:S(2)}, u32[]{:S(2)}) async-start(f32[4,8,64,256]{3,2,1,0:T(8,128)} %pad_maximum_fusion.1), calls=%async_computation.4 | async-start | bytes 4194304 | tf_op jit(solution)/shard_map/all_to_all | solution.py:135
  185.1 52.5 %all-gather.5.cloned.1.call-done = f32[8,8,64,256]{3,2,1,0:T(8,128)} async-done(((f32[1,8,64,256]{3,2,1,0:T(8,128)}), f32[8,8,64,256]{3,2,1,0:T(8,128)}) %all-gather.5.cloned.1.call-update) | async-done | bytes 4194320 | tf_op jit(solution)/shard_map/all_gather | solution.py:14
  237.6 8.5 %while.28 = (s32[]{:T(128)}, f32[8,64,256]{2,1,0:T(8,128)S(1)}, s32[]{:T(128)}, f32[8,8,64,256]{3,2,1,0:T(8,128)}, f32[8,8]{1,0:T(8,128)S(1)}, /*index=5*/s32[]{:T(128)}, s32[]{:T(128)}) while((s32[]{:T(128)}, f32[8,64,256]{2,1,0:T(8,128)S(1)}, s32[]{:T(128)}, f32[8,8,64,256]{3,2,1,0:T(8,128)}, f32[8,8]{1,0:T(8,128)S(1)}, ...), condition=%wide.region_2.3_spmd.clone, body=%wide.region_1.2_spmd.clone.sunk | while | flops 524292 | bytes 1573073 | solution.py:26
  246.1 1.7 add_bitcast_fusion.2
  249.3 4.8 %all-to-all-start.2 = ((f32[4,1,8,64,256]{4,3,2,1,0:T(8,128)}), f32[4,1,8,64,256]{4,3,2,1,0:T(8,128)}, u32[]{:S(2)}, u32[]{:S(2)}) async-start(f32[4,1,8,64,256]{4,3,2,1,0:T(8,128)} %pad_maximum_fusion), calls=%async_computation.2 | async-start | bytes 4194304 | tf_op jit(solution)/shard_map/all_to_all | solution.py:130
  254.1 2.7 fusion.14
  256.8 1.8 copy.106
  258.7 2.3 fusion.24
  261.0 2.1 fusion.28
  263.1 16.5 %all-to-all-done.2 = f32[4,1,8,64,256]{4,3,2,1,0:T(8,128)} async-done(((f32[4,1,8,64,256]{4,3,2,1,0:T(8,128)}), f32[4,1,8,64,256]{4,3,2,1,0:T(8,128)}, u32[]{:S(2)}, u32[]{:S(2)}) %all-to-all-start.2) | async-done | bytes 2097184 | tf_op jit(solution)/shard_map/all_to_all | solution.py:130
  279.6 1.9 copy.94
  287.9 3.2 %fusion.5 = bf16[2,128,8,256]{3,1,2,0:T(8,128)(2,1)} fusion(f32[2,8,256,128]{2,3,1,0:T(8,128)} %fusion.28, f32[2,128,8]{1,2,0:T(8,128)S(1)} %get-tuple-element.264, bf16[2,128,8,256]{3,2,1,0:T(8,128)(2,1)S(1)} %bitcast.293, bf16[2,128,8,256]{3,2,1,0:T(8,128)(2,1)S(1)} %bitcast.286, bf16[2,128,8,256]{3,2,1,0:T(8,128)(2,1)S(1)} %bitcast.297, ...), kind=kOutput, calls=%fused_computation.18 | convolution fusion | flops 271843328 | bytes 6324224 | tf_op jit(solution)/shard_map/bhts,bthe->bshe/dot_general | solution.py:63
  291.1 1.8 copy.117
  (98 shorter events, 33.8 us)
Async XLA Ops:
  7.2 8.1 %copy-start.14 = (bf16[256,2048]{1,0:T(8,128)(2,1)S(1)}, bf16[256,2048]{1,0:T(8,128)(2,1)}, u32[]{:S(2)}) copy-start(bf16[256,2048]{1,0:T(8,128)(2,1)} %param.12) | copy-start | bytes 3145732
  9.3 16.5 %all-to-all-start.1 = ((f32[1,8,4,1]{1,3,0,2:T(1,128)}), f32[1,8,4,1]{1,3,0,2:T(1,128)S(1)}, u32[]{:S(2)}, u32[]{:S(2)}) async-start(f32[1,8,4,1]{1,3,0,2:T(1,128)} %broadcast_in_dim.21), calls=%async_computation.1 | async-start | bytes 4096 | tf_op jit(solution)/shard_map/all_to_all | solution.py:99
  13.6 2.0 copy-start.15
  15.2 2.4 copy-start.4
  15.2 2.0 copy-start.16
  15.6 2.0 copy-start.6
  15.9 3.1 %copy-start.9 = (bf16[32,8,8,256]{3,2,1,0:T(8,128)(2,1)}, bf16[32,8,8,256]{3,2,1,0:T(8,128)(2,1)S(1)}, u32[]{:S(2)}) copy-start(bf16[32,8,8,256]{3,2,1,0:T(8,128)(2,1)S(1)} %copy.132) | copy-start | bytes 3145732
  17.6 1.4 copy-start
  25.8 30.2 %all-to-all-start.3 = ((f32[1,8,256,256]{3,1,0,2:T(8,128)}), f32[1,8,256,256]{3,1,0,2:T(8,128)}, u32[]{:S(2)}, u32[]{:S(2)}) async-start(f32[1,8,256,256]{3,1,0,2:T(8,128)} %copy.103), calls=%async_computation.3 | async-start | bytes 4194304 | tf_op jit(solution)/shard_map/all_to_all | solution.py:101
  56.0 30.2 %all-to-all-start = ((f32[1,8,256,256]{3,1,0,2:T(8,128)}), f32[1,8,256,256]{3,1,0,2:T(8,128)}, u32[]{:S(2)}, u32[]{:S(2)}) async-start(f32[1,8,256,256]{3,1,0,2:T(8,128)} %copy.89), calls=%async_computation | async-start | bytes 4194304 | tf_op jit(solution)/shard_map/all_to_all | solution.py:100
  60.4 103.7 %all-gather.7.cloned.1.call-start = ((), (), s32[]{:S(2)}) async-start(), calls=%async_computation.6 | async-start | bytes 4718592 | tf_op jit(solution)/shard_map/all_gather | solution.py:14
  86.2 2.4 copy-start.3
  88.6 1.7 copy-start.2
  90.3 147.3 %all-gather.5.cloned.1.call-start = ((), (), s32[]{:S(2)}) async-start(), calls=%async_computation.5 | async-start | bytes 4718592 | tf_op jit(solution)/shard_map/all_gather | solution.py:14
  180.6 68.7 %all-to-all-start.4 = ((f32[4,8,64,256]{3,2,1,0:T(8,128)}), f32[4,8,64,256]{3,2,1,0:T(8,128)}, u32[]{:S(2)}, u32[]{:S(2)}) async-start(f32[4,8,64,256]{3,2,1,0:T(8,128)} %pad_maximum_fusion.1), calls=%async_computation.4 | async-start | bytes 4194304 | tf_op jit(solution)/shard_map/all_to_all | solution.py:135
  249.3 4.8 %copy-start.7 = (bf16[32,8,8,256]{3,2,1,0:T(8,128)(2,1)S(1)}, bf16[32,8,8,256]{3,2,1,0:T(8,128)(2,1)}, u32[]{:S(2)}) copy-start(bf16[32,8,8,256]{3,2,1,0:T(8,128)(2,1)} %copy-done.6) | copy-start | bytes 3145732
  249.3 30.3 %all-to-all-start.2 = ((f32[4,1,8,64,256]{4,3,2,1,0:T(8,128)}), f32[4,1,8,64,256]{4,3,2,1,0:T(8,128)}, u32[]{:S(2)}, u32[]{:S(2)}) async-start(f32[4,1,8,64,256]{4,3,2,1,0:T(8,128)} %pad_maximum_fusion), calls=%async_computation.2 | async-start | bytes 4194304 | tf_op jit(solution)/shard_map/all_to_all | solution.py:130
  256.8 1.9 copy-start.10
  258.7 2.3 copy-start.1
  263.1 18.4 %copy-start.8 = (bf16[32,8,8,256]{3,2,1,0:T(8,128)(2,1)S(1)}, bf16[32,8,8,256]{3,2,1,0:T(8,128)(2,1)}, u32[]{:S(2)}) copy-start(bf16[32,8,8,256]{3,2,1,0:T(8,128)(2,1)} %copy-done.6) | copy-start | bytes 3145732
  279.6 2.2 copy-start.11
  281.8 1.0 copy-start.13
  283.4 1.9 copy-start.5
  283.4 1.9 copy-start.12
Sparse Core Ops, SparseCore 0:
  90.4 73.6 all-gather.6
  166.2 71.3 all-gather.4
